TPU v7x, 32 devices: a whole 2x2x4 slice. The times are simulated.
32 devices in a mesh: dp: 8 (over z, core), expert: 4 (over y, x).
Axes of the slice: x: 2, y: 2, z: 4, core: 2. Of those that a mesh axis runs over, the one named last changes fastest.
Arguments:
- attention_gradient: bfloat16 [8, 6144, 1024], P('dp', None, 'expert')
- attention_weight: float32 [6144, 1024], P('dp', 'expert'), may hold values from -6 to 6
- attention_mean: float32 [6144, 1024], P('dp', 'expert'), may hold values from -0.0012 to 0.0012
- attention_square: float32 [6144, 1024], P('dp', 'expert'), may hold values from 1e-09 to 1e-07
- expert_gradient: float32 [8, 4, 8, 6144], P('dp', 'expert')
- expert_weight: float32 [8, 4, 8, 6144], P('dp', 'expert'), may hold values from -6 to 6
- held_mean: float32 [8, 32, 6144], P('dp', 'expert'), may hold values from -0.0006 to 0.0006
- held_square: float32 [8, 32, 6144], P('dp', 'expert'), may hold values from 1e-10 to 1e-08
- live_block_count: int32 [4], replicated, may hold values from 1 to 8, as said below
- holder_table: int32 [4, 8], replicated, may hold values from 0 to 3, as said below
- slot_table: int32 [4, 8], replicated, may hold values from 0 to 7, as said below
- step_count: int32 [1], replicated, may hold values from 1 to 40
Outputs:
- updated_attention: float32 [6144, 1024], P('dp', 'expert')
- updated_means: float32 [6144, 1024], P('dp', 'expert')
- updated_squares: float32 [6144, 1024], P('dp', 'expert')
- updated_experts: float32 [8, 4, 8, 6144], P('dp', 'expert')
- expert_means: float32 [8, 4, 8, 6144], P('dp', 'expert')
- expert_squares: float32 [8, 4, 8, 6144], P('dp', 'expert')
Inputs may be any that keep to these rules, and one draw needn't show every extreme that they name: `live_block_count`: every expert has 1 to 8 live blocks and some expert has exactly 8. `holder_table`: no holder holds more than 2 live blocks of one expert, and some holder holds exactly 2 of one. `slot_table`: the blocks on one holder sit in distinct slots, and some holder has all 8 slots live.
All inputs are finite; a program needn't handle non-finite values.
Results may differ from a plain program's by a relative error of at most 0.0003.
Values sent between devices are 32-bit elements; how exact they have to be, the bound alone decides.
A program may use at most 64 MiB of HBM per device.

v0:
```python
import jax
import jax.numpy as jnp
from jax import lax
from jax.sharding import PartitionSpec as P

MAXB = 8
HSLOTS = 8


beta_first = 0.9
beta_second = 0.95
learn_rate = 0.1
decay_rate = 0.1
adam_epsilon = 1e-08
clip_norm = 1.0


def adam_step(weight, mean, square, gradient, factor, step_float):
    scaled = factor * gradient
    mean_new = beta_first * mean + (1.0 - beta_first) * scaled
    square_new = beta_second * square + (1.0 - beta_second) * scaled * scaled
    mean_hat = mean_new / (1.0 - jnp.power(beta_first, step_float))
    square_hat = square_new / (1.0 - jnp.power(beta_second, step_float))
    weight_new = weight - learn_rate * (
        mean_hat / (jnp.sqrt(square_hat) + adam_epsilon) + decay_rate * weight
    )
    return (weight_new, mean_new, square_new)


def body(
    attention_gradient,
    attention_weight,
    attention_mean,
    attention_square,
    expert_gradient,
    expert_weight,
    held_mean,
    held_square,
    live_block_count,
    holder_table,
    slot_table,
    step_count,
):
    local_gradient = attention_gradient[0]
    experts_all = holder_table.shape[0]
    per_holder = max(1, MAXB // lax.axis_size("expert"))
    block_position = jnp.arange(MAXB, dtype=jnp.int32)
    owner = lax.axis_index("expert")
    expert_pick = jnp.arange(experts_all, dtype=jnp.int32) == owner
    owned_block_count = jnp.sum(jnp.where(expert_pick, live_block_count, 0))
    own_holder = jnp.sum(jnp.where(expert_pick[:, None], holder_table, 0), axis=0)
    live_block_mask = block_position < owned_block_count
    gradient_tiles = expert_gradient[0, 0]
    expert_share = jnp.sum(
        jnp.where(live_block_mask[:, None], gradient_tiles * gradient_tiles, 0.0)
    )
    width = held_mean.shape[2]
    alive_all = block_position[None, :] < live_block_count[:, None]
    minelive = (holder_table == owner) & alive_all
    mine_count = minelive.astype(jnp.int32)
    rank_held = jnp.cumsum(mine_count, axis=1) - mine_count
    places = jnp.arange(per_holder, dtype=jnp.int32)
    slot_ids = jnp.arange(HSLOTS, dtype=jnp.int32)
    selector = jnp.sum(
        (
            minelive[:, :, None, None]
            & (rank_held[:, :, None, None] == places[None, None, :, None])
            & (slot_table[:, :, None, None] == slot_ids[None, None, None, :])
        ).astype(jnp.float32),
        axis=1,
    )
    outgoing_mean = jnp.einsum(
        "oqs,sd->oqd", selector, held_mean[0], precision=lax.Precision.HIGHEST
    )
    outgoing_square = jnp.einsum(
        "oqs,sd->oqd", selector, held_square[0], precision=lax.Precision.HIGHEST
    )
    incoming_mean, incoming_square = (
        lax.all_to_all(outgoing_mean, "expert", split_axis=0, concat_axis=0, tiled=True),
        lax.all_to_all(outgoing_square, "expert", split_axis=0, concat_axis=0, tiled=True),
    )
    earlier = (
        (own_holder[:, None] == own_holder[None, :])
        & live_block_mask[None, :]
        & (block_position[None, :] < block_position[:, None])
    )
    own_rank = jnp.sum(earlier.astype(jnp.int32), axis=1)
    target = own_holder * per_holder + own_rank
    flat_ids = jnp.arange(experts_all * per_holder, dtype=jnp.int32)
    picker = ((target[:, None] == flat_ids[None, :]) & live_block_mask[:, None]).astype(jnp.float32)
    owned_mean = jnp.dot(
        picker,
        incoming_mean.reshape(experts_all * per_holder, width),
        precision=lax.Precision.HIGHEST,
        preferred_element_type=jnp.float32,
    )
    owned_square = jnp.dot(
        picker,
        incoming_square.reshape(experts_all * per_holder, width),
        precision=lax.Precision.HIGHEST,
        preferred_element_type=jnp.float32,
    )
    owned_gradient = lax.psum_scatter(
        local_gradient.astype(jnp.float32), "dp", scatter_dimension=0, tiled=True
    )
    attention_part = jnp.sum(owned_gradient * owned_gradient)
    summed_parts = lax.psum((attention_part, expert_share), ("dp", "expert"))
    total = summed_parts[0] + summed_parts[1]
    factor = jnp.minimum(1.0, clip_norm / (jnp.sqrt(total) + 1e-06))
    step_float = step_count[0].astype(jnp.float32)
    attention_new, means_new, squares_new = adam_step(
        attention_weight, attention_mean, attention_square, owned_gradient, factor, step_float
    )
    weight_blocks = expert_weight[0, 0]
    weight_next, mean_next, square_next = adam_step(
        weight_blocks, owned_mean, owned_square, gradient_tiles, factor, step_float
    )
    live_flags = live_block_mask[:, None]
    experts_new = jnp.where(live_flags, weight_next, weight_blocks)
    means_kept = jnp.where(live_flags, mean_next, 0.0)
    squares_kept = jnp.where(live_flags, square_next, 0.0)
    return (
        attention_new,
        means_new,
        squares_new,
        experts_new[None, None],
        means_kept[None, None],
        squares_kept[None, None],
    )


def solution(mesh):
    placed = (
        P("dp", None, "expert"),
        P("dp", "expert"),
        P("dp", "expert"),
        P("dp", "expert"),
        P("dp", "expert", None, None),
        P("dp", "expert", None, None),
        P("dp", "expert", None),
        P("dp", "expert", None),
        P(),
        P(),
        P(),
        P(),
    )
    return jax.shard_map(
        body,
        mesh=mesh,
        in_specs=placed,
        out_specs=(
            P("dp", "expert"),
            P("dp", "expert"),
            P("dp", "expert"),
            P("dp", "expert", None, None),
            P("dp", "expert", None, None),
            P("dp", "expert", None, None),
        ),
        check_vma=False,
    )
```

profile of v0, /device:TPU:0, one launch (start us, length us, event | category | flops | bytes accessed | tf_op | source)
XLA Modules:
  0.0 138.2 jit_solution(14042447339251599127)
XLA Ops:
  7.2 0.0 copy-start
  7.2 0.0 copy-start.8
  7.2 0.0 copy-start.6
  7.2 0.0 copy-start.7
  7.2 0.0 copy-start.5
  7.2 0.0 reduce-scatter.2.cloned.1.call-start
  7.3 5.2 %bitcast_convert_fusion = f32[6144,256]{1,0:T(8,128)} fusion(bf16[1,6144,256]{2,1,0:T(8,128)(2,1)} %param.12), kind=kLoop, calls=%fused_computation.4 | loop fusion | flops 1572864 | bytes 9437184 | tf_op jit(solution)/shard_map/convert_element_type | solution.py:104
  12.5 0.0 copy-start.4
  12.5 0.0 copy-start.9
  12.5 0.0 copy-start.1
  12.5 0.0 copy-start.2
  12.5 0.0 copy-start.3
  12.5 0.0 reduce-scatter.2.cloned.1.call-update
  12.5 0.0 copy-done.8
  12.5 0.0 copy-done.6
  12.5 0.1 fusion.20
  12.6 0.2 reduce_window_sum.11
  12.8 0.0 copy-done.7
  12.8 0.1 iota_compare_fusion
  12.9 0.1 convert_reduce_fusion
  13.0 0.0 copy-done
  13.0 1.2 fusion.4
  14.2 5.2 %all-to-all-start.1 = ((f32[4,2,6144]{2,1,0:T(2,128)}), f32[4,2,6144]{2,1,0:T(2,128)S(1)}, u32[]{:S(2)}, u32[]{:S(2)}) async-start(f32[4,2,6144]{2,1,0:T(2,128)} %fusion.4), calls=%async_computation.2 | async-start | bytes 393216 | tf_op jit(solution)/shard_map/all_to_all | solution.py:80
  19.4 0.6 select_reduce_fusion.1
  20.0 0.6 iota_compare_fusion.5
  20.7 0.1 select_reduce_fusion
  20.8 0.2 convert_reduce_fusion.1
  21.0 0.0 copy-done.5
  21.0 1.2 fusion.6
  22.2 2.4 %all-to-all-done.1 = f32[4,2,6144]{2,1,0:T(2,128)S(1)} async-done(((f32[4,2,6144]{2,1,0:T(2,128)}), f32[4,2,6144]{2,1,0:T(2,128)S(1)}, u32[]{:S(2)}, u32[]{:S(2)}) %all-to-all-start.1) | async-done | bytes 196640 | tf_op jit(solution)/shard_map/all_to_all | solution.py:80
  24.6 3.4 %all-to-all-start = ((f32[4,2,6144]{2,1,0:T(2,128)}), f32[4,2,6144]{2,1,0:T(2,128)S(1)}, u32[]{:S(2)}, u32[]{:S(2)}) async-start(f32[4,2,6144]{2,1,0:T(2,128)} %fusion.6), calls=%async_computation.1 | async-start | bytes 393216 | tf_op jit(solution)/shard_map/all_to_all | solution.py:79
  28.0 0.0 copy-done.4
  28.0 0.7 fusion.10
  29.4 0.1 reshape.75
  29.6 55.6 %reduce-scatter.2.cloned.1.call-done = f32[768,256]{1,0:T(8,128)} async-done(((f32[6144,256]{1,0:T(8,128)}), f32[768,256]{1,0:T(8,128)}) %reduce-scatter.2.cloned.1.call-update) | async-done | bytes 786448 | tf_op jit(solution)/shard_map/reduce_scatter | solution.py:103
  85.2 1.9 %multiply_reduce_fusion = f32[]{:T(128)} fusion(f32[768,256]{1,0:T(8,128)} %reduce-scatter.2.cloned.1.call-done), kind=kLoop, calls=%fused_computation.9 | loop fusion | flops 393215 | bytes 786436 | tf_op jit(solution)/shard_map/reduce_sum | solution.py:106
  88.4 0.0 all-to-all-done
  88.5 0.1 reshape.74
  88.6 37.7 %psum.16 = f32[]{:T(128)} all-reduce(f32[]{:T(128)S(6)} %add.49), channel_id=1, replica_groups=mesh['dp'=8,'expert'=4] {'dp','expert'}, use_global_device_ids=true, to_apply=%region_2.3 | all-reduce | flops 1 | bytes 8 | tf_op jit(solution)/shard_map/psum | solution.py:107
  127.0 0.3 fusion
  127.3 0.0 copy-done.9
  127.4 1.1 select_bitcast_fusion
  128.5 0.0 copy-done.1
  128.5 0.0 copy-done.2
  128.5 0.0 copy-done.3
  128.5 2.9 %multiply_subtract_fusion = (f32[768,256]{1,0:T(8,128)}, f32[768,256]{1,0:T(8,128)}, f32[768,256]{1,0:T(8,128)}) fusion(f32[768,256]{1,0:T(8,128)S(1)} %copy-done.1, f32[]{:T(128)} %bitcast.3, f32[]{:T(128)} %bitcast.2, f32[768,256]{1,0:T(8,128)} %reduce-scatter.2.cloned.1.call-done, f32[]{:T(128)S(6)} %min.3, f32[768,256]{1,0:T(8,128)S(1)} %copy-done.2, ...), kind=kLoop, calls=%fused_computation.7 | loop fusion | flops 3145728 | bytes 5505036 | tf_op jit(solution)/shard_map/sub | solution.py:24
  (4 shorter events, 0.0 us)
Async XLA Ops:
  7.2 5.8 %copy-start = (f32[1,8,6144]{2,1,0:T(8,128)S(1)}, f32[1,8,6144]{2,1,0:T(8,128)}, u32[]{:S(2)}) copy-start(f32[1,8,6144]{2,1,0:T(8,128)} %param.19) | copy-start | bytes 589828
  7.2 5.3 %copy-start.8 = (s32[4]{0:T(128)S(1)}, s32[4]{0:T(128)}, u32[]{:S(2)}) copy-start(s32[4]{0:T(128)} %param.20) | copy-start | bytes 52
  7.2 5.3 %copy-start.6 = (s32[4,8]{1,0:T(4,128)S(1)}, s32[4,8]{1,0:T(4,128)}, u32[]{:S(2)}) copy-start(s32[4,8]{1,0:T(4,128)} %param.21) | copy-start | bytes 388
  7.2 5.6 %copy-start.7 = (s32[4,8]{1,0:T(4,128)S(1)}, s32[4,8]{1,0:T(4,128)}, u32[]{:S(2)}) copy-start(s32[4,8]{1,0:T(4,128)} %param.22) | copy-start | bytes 388
  7.2 13.8 %copy-start.5 = (f32[1,8,6144]{2,1,0:T(8,128)S(1)}, f32[1,8,6144]{2,1,0:T(8,128)}, u32[]{:S(2)}) copy-start(f32[1,8,6144]{2,1,0:T(8,128)} %param.18) | copy-start | bytes 589828
  7.2 78.0 %reduce-scatter.2.cloned.1.call-start = ((), (), s32[]{:S(2)}) async-start(), calls=%async_computation.3 | async-start | bytes 7077888 | tf_op jit(solution)/shard_map/reduce_scatter | solution.py:103
  12.5 15.5 %copy-start.4 = (f32[1,1,8,6144]{3,2,1,0:T(8,128)S(1)}, f32[1,1,8,6144]{3,2,1,0:T(8,128)}, u32[]{:S(2)}) copy-start(f32[1,1,8,6144]{3,2,1,0:T(8,128)} %param.16) | copy-start | bytes 589828
  12.5 114.9 %copy-start.9 = (f32[1,1,8,6144]{3,2,1,0:T(8,128)S(1)}, f32[1,1,8,6144]{3,2,1,0:T(8,128)}, u32[]{:S(2)}) copy-start(f32[1,1,8,6144]{3,2,1,0:T(8,128)} %param.17) | copy-start | bytes 589828
  12.5 116.0 %copy-start.1 = (f32[768,256]{1,0:T(8,128)S(1)}, f32[768,256]{1,0:T(8,128)}, u32[]{:S(2)}) copy-start(f32[768,256]{1,0:T(8,128)} %param.13) | copy-start | bytes 2359300
  12.5 116.0 %copy-start.2 = (f32[768,256]{1,0:T(8,128)S(1)}, f32[768,256]{1,0:T(8,128)}, u32[]{:S(2)}) copy-start(f32[768,256]{1,0:T(8,128)} %param.15) | copy-start | bytes 2359300
  12.5 116.0 %copy-start.3 = (f32[768,256]{1,0:T(8,128)S(1)}, f32[768,256]{1,0:T(8,128)}, u32[]{:S(2)}) copy-start(f32[768,256]{1,0:T(8,128)} %param.14) | copy-start | bytes 2359300
  14.2 10.4 %all-to-all-start.1 = ((f32[4,2,6144]{2,1,0:T(2,128)}), f32[4,2,6144]{2,1,0:T(2,128)S(1)}, u32[]{:S(2)}, u32[]{:S(2)}) async-start(f32[4,2,6144]{2,1,0:T(2,128)} %fusion.4), calls=%async_computation.2 | async-start | bytes 393216 | tf_op jit(solution)/shard_map/all_to_all | solution.py:80
  24.6 63.9 %all-to-all-start = ((f32[4,2,6144]{2,1,0:T(2,128)}), f32[4,2,6144]{2,1,0:T(2,128)S(1)}, u32[]{:S(2)}, u32[]{:S(2)}) async-start(f32[4,2,6144]{2,1,0:T(2,128)} %fusion.6), calls=%async_computation.1 | async-start | bytes 393216 | tf_op jit(solution)/shard_map/all_to_all | solution.py:79
Sparse Core Ops, SparseCore 0:
  12.6 72.5 reduce-scatter.1
where the time goes:
time: 139 us; the launch traced here: 138 us
  waiting for transfers between devices  58.1 us (42%)
  blocking collectives  37.7 us (27%)
  between operations  17 us (12%)
  other arithmetic  12.7 us (9%)
  starting transfers between devices  8.59 us (6%)
  matrix products  3.85 us (3%)
    reduce_scatter x1, waiting for transfers between devices, body(): lax.psum_scatter(local_gradient.astype(jnp.float32), 'dp', scatter_dimens...  55.6 us
    psum x1, blocking collectives, body(): summed_parts = lax.psum((attention_part, expert_share), ('dp', 'expert'))  37.7 us
    all_to_all x1, starting transfers between devices, body(): lax.all_to_all(outgoing_square, 'expert', split_axis=0, concat_axis=0, ti...  5.19 us
    convert_element_type x1, other arithmetic, body(): local_gradient.astype(jnp.float32)  5.18 us
    all_to_all x1, starting transfers between devices, body(): lax.all_to_all(outgoing_mean, 'expert', split_axis=0, concat_axis=0, tile...  3.37 us
    sub x1, other arithmetic, adam_step(): weight - learn_rate * (mean_hat / (jnp.sqrt(square_hat) + adam_epsilon) +...  2.9 us
  transfers between devices with their start and end apart: 3, of which 2 were waited for; matrix products, arithmetic and copies ran while one was open for 5% of the time, Pallas kernels for 0%

commit v1 on v0

v1 whole, which is shorter than its diff:
```python
import functools

import jax
import jax.numpy as jnp
from jax import lax
from jax.experimental import pallas as pl
from jax.experimental.pallas import tpu as pltpu
from jax.sharding import PartitionSpec as P

MESH = pl.DeviceIdType.MESH
CORES = 2
LAG = 3

beta_first = 0.9
beta_second = 0.95
learn_rate = 0.1
decay_rate = 0.1
adam_epsilon = 1e-08
clip_norm = 1.0


def power(base, exponent):
    result = jnp.float32(1.0)
    value = base
    for bit in range(31):
        factor = value if value > 1e-37 else 0.0
        result = jnp.where((exponent >> bit) & 1 == 1, result * jnp.float32(factor), result)
        value = value * value
    return result


def adam_step(weight, mean, square, gradient, factor, first_scale, second_scale):
    scaled = factor * gradient
    mean_new = beta_first * mean + (1.0 - beta_first) * scaled
    square_new = beta_second * square + (1.0 - beta_second) * scaled * scaled
    mean_hat = mean_new * first_scale
    square_hat = square_new * second_scale
    weight_new = weight - learn_rate * (
        mean_hat / (jnp.sqrt(square_hat) + adam_epsilon) + decay_rate * weight
    )
    return weight_new, mean_new, square_new


def kernel(
    levels, experts, pieces, per_holder,
    grad_hbm, w_hbm, m_hbm, v_hbm, eg_hbm, ew_hbm, hm_hbm, hs_hbm,
    count_ref, holder_ref, slot_ref, step_ref,
    ow_ref, om_ref, ov_ref, oew_ref, oem_ref, oes_ref,
    grad, pair_out, local, recv, w_in, m_in, v_in, eg, ew, hm, hs,
    out_mean, out_square, in_mean, in_square, own_mean, own_square, part, parts,
    grad_sem, load_sem, pair_send, pair_recv, link_send, link_recv,
    mom_send, mom_recv, part_send, part_recv,
):
    dp = lax.axis_index("dp")
    me = lax.axis_index("expert")
    z = dp // CORES
    core = dp % CORES
    other = 1 - core
    partner = z * CORES + other
    upper = 2 * z >= levels
    maxb = holder_ref.shape[1]
    total_pieces = levels * pieces
    devices = levels * CORES * experts

    def level_of(j):
        return jnp.where(upper, j, levels - 1 - j)

    def grad_load(j):
        d = level_of(j)
        return pltpu.make_async_copy(grad_hbm.at[d], grad.at[d], grad_sem.at[j])

    for j in range(levels):
        grad_load(j).start()
    loads = [
        pltpu.make_async_copy(a, b, load_sem.at[i])
        for i, (a, b) in enumerate(
            ((hm_hbm, hm), (hs_hbm, hs), (eg_hbm, eg), (ew_hbm, ew), (w_hbm, w_in), (m_hbm, m_in), (v_hbm, v_in))
        )
    ]
    for load in loads:
        load.start()

    barrier = pltpu.get_barrier_semaphore()
    pl.semaphore_signal(barrier, inc=1, device_id=(partner, me), device_id_type=MESH)
    for off in range(1, experts):
        pl.semaphore_signal(barrier, inc=1, device_id=(dp, lax.rem(me + off, experts)), device_id_type=MESH)

    @pl.when(z > 0)
    def _():
        pl.semaphore_signal(barrier, inc=1, device_id=(dp - CORES, me), device_id_type=MESH)

    @pl.when(z < levels - 1)
    def _():
        pl.semaphore_signal(barrier, inc=1, device_id=(dp + CORES, me), device_id_type=MESH)

    near = jnp.where(z > 0, 1, 0) + jnp.where(z < levels - 1, 1, 0)
    pl.semaphore_wait(barrier, experts + near)

    def pair_copy(d, p):
        return pltpu.make_async_remote_copy(
            src_ref=pair_out.at[d, p], dst_ref=local.at[d, p],
            send_sem=pair_send.at[d * pieces + p], recv_sem=pair_recv.at[d * pieces + p],
            device_id=(partner, me), device_id_type=MESH,
        )

    def link_copy(way, d, p, src):
        return pltpu.make_async_remote_copy(
            src_ref=src, dst_ref=recv.at[way, d, p],
            send_sem=link_send.at[way, d * pieces + p], recv_sem=link_recv.at[way, d * pieces + p],
            device_id=(jnp.where(way == 0, dp + CORES, dp - CORES), me), device_id_type=MESH,
        )

    def give(j):
        grad_load(j).wait()
        d = level_of(j)

        @pl.loop(0, pieces)
        def _(p):
            pair_out[d, p] = grad[d, other, p].astype(jnp.float32)
            pair_copy(d, p).start()

    way_out = jnp.where(upper, 1, 0)
    at_end = (z == 0) | (z == levels - 1)

    def take(j):
        d = level_of(j)

        @pl.loop(0, pieces)
        def _(p):
            pair_copy(d, p).wait_recv()
            local[d, p] = local[d, p] + grad[d, core, p].astype(jnp.float32)

            @pl.when(at_end & (d != z))
            def _():
                link_copy(way_out, d, p, local.at[d, p]).start()

    give(0)

    @pl.loop(0, levels)
    def _(j):
        @pl.when(j + 1 < levels)
        def _():
            give(j + 1)

        take(j)

    loads[0].wait()
    loads[1].wait()

    def moment_copy(which, src, dst, target, source):
        return pltpu.make_async_remote_copy(
            src_ref=src.at[target], dst_ref=dst.at[source],
            send_sem=mom_send.at[which, target], recv_sem=mom_recv.at[which, source],
            device_id=(dp, target), device_id_type=MESH,
        )

    def picks(owner):
        rank = jnp.int32(0)
        chosen = [jnp.int32(0)] * per_holder
        for b in range(maxb):
            mine = (holder_ref[owner, b] == me) & (b < count_ref[owner])
            for q in range(per_holder):
                chosen[q] = jnp.where(mine & (rank == q), slot_ref[owner, b], chosen[q])
            rank = rank + jnp.where(mine, 1, 0)
        return chosen

    for q, slot in enumerate(picks(me)):
        in_mean[me, pl.ds(q, 1), :] = hm[pl.ds(slot, 1), :]
        in_square[me, pl.ds(q, 1), :] = hs[pl.ds(slot, 1), :]

    @pl.loop(1, experts)
    def _(off):
        owner = lax.rem(me + off, experts)
        for q, slot in enumerate(picks(owner)):
            out_mean[owner, pl.ds(q, 1), :] = hm[pl.ds(slot, 1), :]
            out_square[owner, pl.ds(q, 1), :] = hs[pl.ds(slot, 1), :]
        moment_copy(0, out_mean, in_mean, owner, me).start()
        moment_copy(1, out_square, in_square, owner, me).start()

    def forward(way, k):
        j = k // pieces
        p = k % pieces
        d = jnp.where(way == 0, levels - 1 - j, j)
        ahead = jnp.where(way == 0, (d > z) & (z > 0), (d < z) & (z < levels - 1))

        @pl.when(ahead)
        def _():
            copy = link_copy(way, d, p, recv.at[way, d, p])
            copy.wait_recv()
            recv[way, d, p] = recv[way, d, p] + local[d, p]
            copy.start()

    @pl.loop(0, total_pieces + LAG)
    def _(s):
        @pl.when(s < total_pieces)
        def _():
            forward(way_out, s)

        @pl.when(s >= LAG)
        def _():
            forward(1 - way_out, s - LAG)

    @pl.loop(1, experts)
    def _(off):
        source = lax.rem(me + off, experts)
        moment_copy(0, out_mean, in_mean, source, source).wait()
        moment_copy(1, out_square, in_square, source, source).wait()

    owned = count_ref[me]
    for b in range(maxb):
        holder = holder_ref[me, b]
        rank = jnp.int32(0)
        for earlier in range(b):
            rank = rank + jnp.where((holder_ref[me, earlier] == holder) & (earlier < owned), 1, 0)
        rank = jnp.minimum(rank, per_holder - 1)
        own_mean[pl.ds(b, 1), :] = in_mean[holder, pl.ds(rank, 1), :]
        own_square[pl.ds(b, 1), :] = in_square[holder, pl.ds(rank, 1), :]
    for load in loads[2:]:
        load.wait()
    width = eg.shape[1]
    live = lax.broadcasted_iota(jnp.int32, (maxb, 128), 0) < owned
    acc = jnp.zeros((maxb, 128), jnp.float32)
    for i in range(width // 128):
        g = eg[:, pl.ds(i * 128, 128)]
        acc = acc + jnp.where(live, g * g, 0.0)
    row = jnp.sum(acc, axis=0, keepdims=True)

    def finish(p, row):
        @pl.when(z < levels - 1)
        def _():
            link_copy(1, z, p, recv.at[1, z, p]).wait_recv()
            local[z, p] = local[z, p] + recv[1, z, p]

        @pl.when(z > 0)
        def _():
            link_copy(0, z, p, recv.at[0, z, p]).wait_recv()
            local[z, p] = local[z, p] + recv[0, z, p]

        g = local[z, p]
        col = jnp.sum(g * g, axis=0, keepdims=True)
        for i in range(g.shape[1] // 128):
            row = row + col[:, i * 128:(i + 1) * 128]
        return row

    row = lax.fori_loop(0, pieces, finish, row)

    index = dp * experts + me
    part[...] = row
    parts[index] = row

    def part_copy(off):
        target = lax.rem(index + off, devices)
        return pltpu.make_async_remote_copy(
            src_ref=part, dst_ref=parts.at[index],
            send_sem=part_send.at[off], recv_sem=part_recv,
            device_id=(target // experts, lax.rem(target, experts)), device_id_type=MESH,
        )

    @pl.loop(1, devices)
    def _(off):
        part_copy(off).start()

    step = step_ref[0]
    one = jnp.ones((1, 1), jnp.float32)
    first_scale = 1.0 / (one * (1.0 - power(beta_first, step)))
    second_scale = 1.0 / (one * (1.0 - power(beta_second, step)))
    others = parts.at[pl.ds(0, devices - 1)]
    pltpu.make_async_copy(others, others, part_recv).wait()
    total = jnp.sum(jnp.sum(parts[...], axis=0), axis=1, keepdims=True)
    factor = jnp.minimum(1.0, clip_norm / (jnp.sqrt(total) + 1e-06))

    @pl.loop(0, pieces)
    def _(p):
        w_new, m_new, v_new = adam_step(
            w_in[p], m_in[p], v_in[p], local[z, p], factor, first_scale, second_scale
        )
        ow_ref[p] = w_new
        om_ref[p] = m_new
        ov_ref[p] = v_new

    for i in range(width // 128):
        cols = pl.ds(i * 128, 128)
        w_old = ew[:, cols]
        w_new, m_new, v_new = adam_step(
            w_old, jnp.where(live, own_mean[:, cols], 0.0), jnp.where(live, own_square[:, cols], 0.0),
            eg[:, cols], factor, first_scale, second_scale,
        )
        oew_ref[:, cols] = jnp.where(live, w_new, w_old)
        oem_ref[:, cols] = jnp.where(live, m_new, 0.0)
        oes_ref[:, cols] = jnp.where(live, v_new, 0.0)

    @pl.loop(1, devices)
    def _(off):
        part_copy(off).wait_send()

    @pl.loop(0, total_pieces)
    def _(k):
        d = k // pieces
        p = k % pieces
        pair_copy(d, p).wait_send()

        @pl.when(d > z)
        def _():
            link_copy(0, d, p, local.at[d, p]).wait_send()

        @pl.when(d < z)
        def _():
            link_copy(1, d, p, local.at[d, p]).wait_send()


def piece_rows(rows):
    for size in range(96, 0, -16):
        if rows % size == 0:
            return size
    return rows


def make_body(mesh):
    n_dp = mesh.shape["dp"]
    experts = mesh.shape["expert"]
    levels = n_dp // CORES

    def body(ag, aw, am, av, eg, ew, hm, hs, count, holder, slot, step):
        depth, cols = ag.shape[1], ag.shape[2]
        rows = depth // n_dp
        size = piece_rows(rows)
        pieces = rows // size
        maxb, width = eg.shape[2], eg.shape[3]
        slots = hm.shape[1]
        per_holder = max(1, maxb // experts)
        f32 = jnp.float32
        own = (pieces, size, cols)
        k = levels * pieces
        dma = pltpu.SemaphoreType.DMA
        hbm = pl.BlockSpec(memory_space=pltpu.HBM)
        smem = pl.BlockSpec(memory_space=pltpu.SMEM)
        vmem = pl.BlockSpec(memory_space=pltpu.VMEM)
        outs = pl.pallas_call(
            functools.partial(kernel, levels, experts, pieces, per_holder),
            out_shape=[jax.ShapeDtypeStruct(own, f32)] * 3 + [jax.ShapeDtypeStruct((maxb, width), f32)] * 3,
            in_specs=[hbm] * 8 + [smem] * 4,
            out_specs=[vmem] * 6,
            scratch_shapes=[
                pltpu.VMEM((levels, CORES, pieces, size, cols), ag.dtype),
                pltpu.VMEM((levels, pieces, size, cols), f32),
                pltpu.VMEM((levels, pieces, size, cols), f32),
                pltpu.VMEM((2, levels, pieces, size, cols), f32),
                pltpu.VMEM(own, f32), pltpu.VMEM(own, f32), pltpu.VMEM(own, f32),
                pltpu.VMEM((maxb, width), f32), pltpu.VMEM((maxb, width), f32),
                pltpu.VMEM((slots, width), f32), pltpu.VMEM((slots, width), f32),
                pltpu.VMEM((experts, per_holder, width), f32), pltpu.VMEM((experts, per_holder, width), f32),
                pltpu.VMEM((experts, per_holder, width), f32), pltpu.VMEM((experts, per_holder, width), f32),
                pltpu.VMEM((maxb, width), f32), pltpu.VMEM((maxb, width), f32),
                pltpu.VMEM((1, 128), f32), pltpu.VMEM((n_dp * experts, 1, 128), f32),
                dma((levels,)), dma((7,)), dma((k,)), dma((k,)), dma((2, k)), dma((2, k)),
                dma((2, experts)), dma((2, experts)), dma((n_dp * experts,)), dma(()),
            ],
            compiler_params=pltpu.CompilerParams(
                collective_id=0, has_side_effects=True, vmem_limit_bytes=40 * 1024 * 1024
            ),
        )(
            ag.reshape(levels, CORES, pieces, size, cols),
            aw.reshape(own), am.reshape(own), av.reshape(own),
            eg[0, 0], ew[0, 0], hm[0], hs[0], count, holder, slot, step,
        )
        return tuple(o.reshape(rows, cols) for o in outs[:3]) + tuple(o[None, None] for o in outs[3:])

    return body


def solution(mesh):
    matrix = P("dp", "expert")
    blocks = P("dp", "expert", None, None)
    held = P("dp", "expert", None)
    return jax.shard_map(
        make_body(mesh),
        mesh=mesh,
        in_specs=(P("dp", None, "expert"), matrix, matrix, matrix, blocks, blocks, held, held, P(), P(), P(), P()),
        out_specs=(matrix, matrix, matrix, blocks, blocks, blocks),
        check_vma=False,
    )
```

time: 139 us -> 86.4 us (0.62)
  Pallas kernels: 0 us -> 69 us
  waiting for transfers between devices: 58.1 us -> 0 us
  blocking collectives: 37.7 us -> 0 us
  between operations: 17 us -> 1.31 us
  local copies, waits for them, and re-layouts: 0.32 us -> 15.7 us
  other arithmetic: 12.7 us -> 0 us
  starting transfers between devices: 8.59 us -> 0 us
  matrix products: 3.85 us -> 0 us
    pallas_call x0 -> x1, Pallas kernels: none -> 69 us  [body(): pl.pallas_call(functools.partial(kernel, levels, experts, pieces, per_hol...]
    reduce_scatter x1 -> x0, waiting for transfers between devices: 55.6 us -> none  [body(): lax.psum_scatter(local_gradient.astype(jnp.float32), 'dp', scatter_dimens...]
    psum x1 -> x0, blocking collectives: 37.7 us -> none  [body(): summed_parts = lax.psum((attention_part, expert_share), ('dp', 'expert'))]
    unnamed x20 -> x28, local copies, waits for them, and re-layouts: 0.05 us -> 15.7 us
    all_to_all x2 -> x0, starting transfers between devices: 8.56 us -> none  [the longest x1 5.19 us: body(): lax.all_to_all(outgoing_square, 'expert', split_axis=0, concat_axis=0, ti...]
    convert_element_type x2 -> x0, other arithmetic: 5.26 us -> none  [the longest x1 5.18 us: body(): local_gradient.astype(jnp.float32)]
    dot_general x4 -> x0, matrix products: 3.85 us -> none  [the longest x1 1.22 us: body(): jnp.einsum('oqs,sd->oqd', selector, held_mean[0], precision=lax.Precision...]
    reduce_sum x6 -> x0, other arithmetic: 3.65 us -> none  [the longest x1 1.94 us: body(): attention_part = jnp.sum(owned_gradient * owned_gradient)]
  transfers between devices with their start and end apart: 3 -> 0, of which waited for: 2 -> 0; matrix products, arithmetic and copies ran while one was open for 5% -> 0% of each run, Pallas kernels for 0% -> 0%
where the time goes in v1:
time: 86.4 us; the launch traced here: 85.9 us
  Pallas kernels  69 us (80%)
  local copies, waits for them, and re-layouts  15.7 us (18%)
  between operations  1.31 us (2%)
    pallas_call x1, Pallas kernels, body(): pl.pallas_call(functools.partial(kernel, levels, experts, pieces, per_hol...  69 us
    unnamed x28, local copies, waits for them, and re-layouts  15.7 us

profile of v1, /device:TPU:0, one launch (start us, length us, event | category | flops | bytes accessed | tf_op | source)
XLA Modules:
  0.0 85.9 jit_solution(14738045349712078519)
XLA Ops:
  1.3 0.0 copy-start
  1.3 1.9 %copy-done = bf16[1,6144,256]{2,1,0:T(8,128)(2,1)S(1)} copy-done((bf16[1,6144,256]{2,1,0:T(8,128)(2,1)S(1)}, bf16[1,6144,256]{2,1,0:T(8,128)(2,1)}, u32[]{:S(2)}) %copy-start) | copy-done | bytes 3145752
  3.2 0.0 copy-start.1
  3.2 1.1 %copy-done.1 = f32[768,256]{1,0:T(8,128)S(1)} copy-done((f32[768,256]{1,0:T(8,128)S(1)}, f32[768,256]{1,0:T(8,128)}, u32[]{:S(2)}) %copy-start.1) | copy-done | bytes 786456
  4.3 0.0 copy-start.2
  4.3 1.1 %copy-done.2 = f32[768,256]{1,0:T(8,128)S(1)} copy-done((f32[768,256]{1,0:T(8,128)S(1)}, f32[768,256]{1,0:T(8,128)}, u32[]{:S(2)}) %copy-start.2) | copy-done | bytes 786456
  5.4 0.0 copy-start.3
  5.4 1.1 %copy-done.3 = f32[768,256]{1,0:T(8,128)S(1)} copy-done((f32[768,256]{1,0:T(8,128)S(1)}, f32[768,256]{1,0:T(8,128)}, u32[]{:S(2)}) %copy-start.3) | copy-done | bytes 786456
  6.6 0.0 copy-start.4
  6.6 0.9 %copy-done.4 = f32[1,1,8,6144]{3,2,1,0:T(8,128)S(1)} copy-done((f32[1,1,8,6144]{3,2,1,0:T(8,128)S(1)}, f32[1,1,8,6144]{3,2,1,0:T(8,128)}, u32[]{:S(2)}) %copy-start.4) | copy-done | bytes 196632
  7.5 0.0 copy-start.5
  7.5 0.9 %copy-done.5 = f32[1,1,8,6144]{3,2,1,0:T(8,128)S(1)} copy-done((f32[1,1,8,6144]{3,2,1,0:T(8,128)S(1)}, f32[1,1,8,6144]{3,2,1,0:T(8,128)}, u32[]{:S(2)}) %copy-start.5) | copy-done | bytes 196632
  8.4 0.0 copy-start.6
  8.4 0.9 %copy-done.6 = f32[1,8,6144]{2,1,0:T(8,128)S(1)} copy-done((f32[1,8,6144]{2,1,0:T(8,128)S(1)}, f32[1,8,6144]{2,1,0:T(8,128)}, u32[]{:S(2)}) %copy-start.6) | copy-done | bytes 196632
  9.4 0.0 copy-start.7
  9.4 0.9 %copy-done.7 = f32[1,8,6144]{2,1,0:T(8,128)S(1)} copy-done((f32[1,8,6144]{2,1,0:T(8,128)S(1)}, f32[1,8,6144]{2,1,0:T(8,128)}, u32[]{:S(2)}) %copy-start.7) | copy-done | bytes 196632
  10.3 0.0 copy-start.8
  10.3 0.7 copy-done.8
  11.0 0.0 copy-start.9
  11.0 0.7 copy-done.9
  11.6 0.0 copy-start.10
  11.7 0.7 copy-done.10
  12.3 69.0 %shard_map.163 = (f32[8,96,256]{2,1,0:T(8,128)S(1)}, f32[8,96,256]{2,1,0:T(8,128)S(1)}, f32[8,96,256]{2,1,0:T(8,128)S(1)}, f32[8,6144]{1,0:T(8,128)S(1)}, f32[8,6144]{1,0:T(8,128)S(1)}, /*index=5*/f32[8,6144]{1,0:T(8,128)S(1)}) custom-call(bf16[4,2,8,96,256]{4,3,2,1,0:T(8,128)(2,1)S(1)} %bitcast.14, f32[8,96,256]{2,1,0:T(8,128)S(1)} %bitcast.15, ...), custom_call_target="tpu_custom_call" | custom-call | tf_op jit(solution)/shard_map/pallas_call | solution.py:338
  81.3 0.9 %copy.25 = f32[768,256]{1,0:T(8,128)} copy(f32[768,256]{1,0:T(8,128)S(1)} %bitcast.20) | data formatting | bytes 1572864
  82.1 0.9 %copy.26 = f32[768,256]{1,0:T(8,128)} copy(f32[768,256]{1,0:T(8,128)S(1)} %bitcast.19) | data formatting | bytes 1572864
  83.0 0.9 %copy.27 = f32[768,256]{1,0:T(8,128)} copy(f32[768,256]{1,0:T(8,128)S(1)} %bitcast.18) | data formatting | bytes 1572864
  83.9 0.7 copy.28
  84.6 0.7 copy.29
  85.3 0.7 copy.30
Async XLA Ops:
  1.3 1.9 %copy-start = (bf16[1,6144,256]{2,1,0:T(8,128)(2,1)S(1)}, bf16[1,6144,256]{2,1,0:T(8,128)(2,1)}, u32[]{:S(2)}) copy-start(bf16[1,6144,256]{2,1,0:T(8,128)(2,1)} %param.12) | copy-start | bytes 9437188
  3.2 1.1 %copy-start.1 = (f32[768,256]{1,0:T(8,128)S(1)}, f32[768,256]{1,0:T(8,128)}, u32[]{:S(2)}) copy-start(f32[768,256]{1,0:T(8,128)} %param.13) | copy-start | bytes 2359300
  4.3 1.1 %copy-start.2 = (f32[768,256]{1,0:T(8,128)S(1)}, f32[768,256]{1,0:T(8,128)}, u32[]{:S(2)}) copy-start(f32[768,256]{1,0:T(8,128)} %param.14) | copy-start | bytes 2359300
  5.4 1.1 %copy-start.3 = (f32[768,256]{1,0:T(8,128)S(1)}, f32[768,256]{1,0:T(8,128)}, u32[]{:S(2)}) copy-start(f32[768,256]{1,0:T(8,128)} %param.15) | copy-start | bytes 2359300
  6.6 0.9 %copy-start.4 = (f32[1,1,8,6144]{3,2,1,0:T(8,128)S(1)}, f32[1,1,8,6144]{3,2,1,0:T(8,128)}, u32[]{:S(2)}) copy-start(f32[1,1,8,6144]{3,2,1,0:T(8,128)} %param.16) | copy-start | bytes 589828
  7.5 0.9 %copy-start.5 = (f32[1,1,8,6144]{3,2,1,0:T(8,128)S(1)}, f32[1,1,8,6144]{3,2,1,0:T(8,128)}, u32[]{:S(2)}) copy-start(f32[1,1,8,6144]{3,2,1,0:T(8,128)} %param.17) | copy-start | bytes 589828
  8.4 0.9 %copy-start.6 = (f32[1,8,6144]{2,1,0:T(8,128)S(1)}, f32[1,8,6144]{2,1,0:T(8,128)}, u32[]{:S(2)}) copy-start(f32[1,8,6144]{2,1,0:T(8,128)} %param.18) | copy-start | bytes 589828
  9.4 0.9 %copy-start.7 = (f32[1,8,6144]{2,1,0:T(8,128)S(1)}, f32[1,8,6144]{2,1,0:T(8,128)}, u32[]{:S(2)}) copy-start(f32[1,8,6144]{2,1,0:T(8,128)} %param.19) | copy-start | bytes 589828
  10.3 0.7 copy-start.8
  11.0 0.7 copy-start.9
  11.6 0.7 copy-start.10

commit v2 on v1

--- a/solution.py
+++ b/solution.py
@@ -10,6 +10,7 @@
 MESH = pl.DeviceIdType.MESH
 CORES = 2
 LAG = 3
+LIMIT = 40 * 1024 * 1024
 
 beta_first = 0.9
 beta_second = 0.95
@@ -43,11 +44,10 @@
 
 def kernel(
     levels, experts, pieces, per_holder,
-    grad_hbm, w_hbm, m_hbm, v_hbm, eg_hbm, ew_hbm, hm_hbm, hs_hbm,
-    count_ref, holder_ref, slot_ref, step_ref,
-    ow_ref, om_ref, ov_ref, oew_ref, oem_ref, oes_ref,
-    grad, pair_out, local, recv, w_in, m_in, v_in, eg, ew, hm, hs,
-    out_mean, out_square, in_mean, in_square, own_mean, own_square, part, parts,
+    grad_hbm, eg_hbm, hm_hbm, hs_hbm, count_hbm, holder_hbm, slot_hbm, step_ref,
+    sum_ref, own_mean, own_square, scale_ref, live_ref,
+    grad, pair_out, local, recv, eg, hm, hs,
+    out_mean, out_square, in_mean, in_square, part, parts, count_ref, holder_ref, slot_ref,
     grad_sem, load_sem, pair_send, pair_recv, link_send, link_recv,
     mom_send, mom_recv, part_send, part_recv,
 ):
@@ -74,7 +74,10 @@
     loads = [
         pltpu.make_async_copy(a, b, load_sem.at[i])
         for i, (a, b) in enumerate(
-            ((hm_hbm, hm), (hs_hbm, hs), (eg_hbm, eg), (ew_hbm, ew), (w_hbm, w_in), (m_hbm, m_in), (v_hbm, v_in))
+            (
+                (count_hbm, count_ref), (holder_hbm, holder_ref), (slot_hbm, slot_ref),
+                (hm_hbm, hm), (hs_hbm, hs), (eg_hbm, eg),
+            )
         )
     ]
     for load in loads:
@@ -92,6 +95,13 @@
     @pl.when(z < levels - 1)
     def _():
         pl.semaphore_signal(barrier, inc=1, device_id=(dp + CORES, me), device_id_type=MESH)
+
+    first = level_of(0)
+    grad_load(0).wait()
+
+    @pl.loop(0, pieces)
+    def _(p):
+        pair_out[first, p] = grad[first, other, p].astype(jnp.float32)
 
     near = jnp.where(z > 0, 1, 0) + jnp.where(z < levels - 1, 1, 0)
     pl.semaphore_wait(barrier, experts + near)
@@ -134,7 +144,9 @@
             def _():
                 link_copy(way_out, d, p, local.at[d, p]).start()
 
-    give(0)
+    @pl.loop(0, pieces)
+    def _(p):
+        pair_copy(first, p).start()
 
     @pl.loop(0, levels)
     def _(j):
@@ -144,8 +156,8 @@
 
         take(j)
 
-    loads[0].wait()
-    loads[1].wait()
+    for load in loads[:5]:
+        load.wait()
 
     def moment_copy(which, src, dst, target, source):
         return pltpu.make_async_remote_copy(
@@ -215,8 +227,7 @@
         rank = jnp.minimum(rank, per_holder - 1)
         own_mean[pl.ds(b, 1), :] = in_mean[holder, pl.ds(rank, 1), :]
         own_square[pl.ds(b, 1), :] = in_square[holder, pl.ds(rank, 1), :]
-    for load in loads[2:]:
-        load.wait()
+    loads[5].wait()
     width = eg.shape[1]
     live = lax.broadcasted_iota(jnp.int32, (maxb, 128), 0) < owned
     acc = jnp.zeros((maxb, 128), jnp.float32)
@@ -224,19 +235,34 @@
         g = eg[:, pl.ds(i * 128, 128)]
         acc = acc + jnp.where(live, g * g, 0.0)
     row = jnp.sum(acc, axis=0, keepdims=True)
+    live_ref[...] = jnp.where(live, 1.0, 0.0)
+    step = step_ref[0]
+    one = jnp.ones((1, 128), jnp.float32)
+    scale_ref[1:2] = 1.0 / (one * (1.0 - power(beta_first, step)))
+    scale_ref[2:3] = 1.0 / (one * (1.0 - power(beta_second, step)))
 
     def finish(p, row):
+        sum_ref[p] = local[z, p]
+
         @pl.when(z < levels - 1)
         def _():
             link_copy(1, z, p, recv.at[1, z, p]).wait_recv()
-            local[z, p] = local[z, p] + recv[1, z, p]
-
-        @pl.when(z > 0)
+
+            @pl.when(z > 0)
+            def _():
+                link_copy(0, z, p, recv.at[0, z, p]).wait_recv()
+                sum_ref[p] = local[z, p] + (recv[0, z, p] + recv[1, z, p])
+
+            @pl.when(z == 0)
+            def _():
+                sum_ref[p] = local[z, p] + recv[1, z, p]
+
+        @pl.when((z == levels - 1) & (z > 0))
         def _():
             link_copy(0, z, p, recv.at[0, z, p]).wait_recv()
-            local[z, p] = local[z, p] + recv[0, z, p]
-
-        g = local[z, p]
+            sum_ref[p] = local[z, p] + recv[0, z, p]
+
+        g = sum_ref[p]
         col = jnp.sum(g * g, axis=0, keepdims=True)
         for i in range(g.shape[1] // 128):
             row = row + col[:, i * 128:(i + 1) * 128]
@@ -260,24 +286,58 @@
     def _(off):
         part_copy(off).start()
 
-    step = step_ref[0]
-    one = jnp.ones((1, 1), jnp.float32)
-    first_scale = 1.0 / (one * (1.0 - power(beta_first, step)))
-    second_scale = 1.0 / (one * (1.0 - power(beta_second, step)))
+    @pl.loop(0, total_pieces)
+    def _(k):
+        d = k // pieces
+        p = k % pieces
+        pair_copy(d, p).wait_send()
+
+        @pl.when(d > z)
+        def _():
+            link_copy(0, d, p, local.at[d, p]).wait_send()
+
+        @pl.when(d < z)
+        def _():
+            link_copy(1, d, p, local.at[d, p]).wait_send()
+
     others = parts.at[pl.ds(0, devices - 1)]
     pltpu.make_async_copy(others, others, part_recv).wait()
     total = jnp.sum(jnp.sum(parts[...], axis=0), axis=1, keepdims=True)
-    factor = jnp.minimum(1.0, clip_norm / (jnp.sqrt(total) + 1e-06))
+    scale_ref[0:1] = jnp.broadcast_to(jnp.minimum(1.0, clip_norm / (jnp.sqrt(total) + 1e-06)), (1, 128))
+
+    @pl.loop(1, devices)
+    def _(off):
+        part_copy(off).wait_send()
+
+
+def update(
+    w_in, m_in, v_in, sums, eg, ew, own_mean, own_square, scale_ref, live_ref,
+    ow_hbm, om_hbm, ov_hbm, oew_hbm, oem_hbm, oes_hbm,
+    ow, om, ov, oew, oem, oes, sem, expert_sem,
+):
+    factor = scale_ref[0:1, 0:1]
+    first_scale = scale_ref[1:2, 0:1]
+    second_scale = scale_ref[2:3, 0:1]
+    pieces = w_in.shape[0]
+    triples = ((ow, ow_hbm), (om, om_hbm), (ov, ov_hbm))
+
+    def put(i, p):
+        src, dst = triples[i]
+        return pltpu.make_async_copy(src.at[p], dst.at[p], sem.at[i, p])
 
     @pl.loop(0, pieces)
     def _(p):
         w_new, m_new, v_new = adam_step(
-            w_in[p], m_in[p], v_in[p], local[z, p], factor, first_scale, second_scale
-        )
-        ow_ref[p] = w_new
-        om_ref[p] = m_new
-        ov_ref[p] = v_new
-
+            w_in[p], m_in[p], v_in[p], sums[p], factor, first_scale, second_scale
+        )
+        ow[p] = w_new
+        om[p] = m_new
+        ov[p] = v_new
+        for i in range(3):
+            put(i, p).start()
+
+    maxb, width = eg.shape
+    live = live_ref[...] > 0.5
     for i in range(width // 128):
         cols = pl.ds(i * 128, 128)
         w_old = ew[:, cols]
@@ -285,27 +345,23 @@
             w_old, jnp.where(live, own_mean[:, cols], 0.0), jnp.where(live, own_square[:, cols], 0.0),
             eg[:, cols], factor, first_scale, second_scale,
         )
-        oew_ref[:, cols] = jnp.where(live, w_new, w_old)
-        oem_ref[:, cols] = jnp.where(live, m_new, 0.0)
-        oes_ref[:, cols] = jnp.where(live, v_new, 0.0)
-
-    @pl.loop(1, devices)
-    def _(off):
-        part_copy(off).wait_send()
-
-    @pl.loop(0, total_pieces)
-    def _(k):
-        d = k // pieces
-        p = k % pieces
-        pair_copy(d, p).wait_send()
-
-        @pl.when(d > z)
-        def _():
-            link_copy(0, d, p, local.at[d, p]).wait_send()
-
-        @pl.when(d < z)
-        def _():
-            link_copy(1, d, p, local.at[d, p]).wait_send()
+        oew[:, cols] = jnp.where(live, w_new, w_old)
+        oem[:, cols] = jnp.where(live, m_new, 0.0)
+        oes[:, cols] = jnp.where(live, v_new, 0.0)
+    rest = [
+        pltpu.make_async_copy(a, b, expert_sem.at[i])
+        for i, (a, b) in enumerate(((oew, oew_hbm), (oem, oem_hbm), (oes, oes_hbm)))
+    ]
+    for copy in rest:
+        copy.start()
+
+    @pl.loop(0, pieces)
+    def _(p):
+        for i in range(3):
+            put(i, p).wait()
+
+    for copy in rest:
+        copy.wait()
 
 
 def piece_rows(rows):
@@ -333,35 +389,50 @@
         k = levels * pieces
         dma = pltpu.SemaphoreType.DMA
         hbm = pl.BlockSpec(memory_space=pltpu.HBM)
-        smem = pl.BlockSpec(memory_space=pltpu.SMEM)
         vmem = pl.BlockSpec(memory_space=pltpu.VMEM)
-        outs = pl.pallas_call(
+        blocks = (maxb, width)
+        shape = jax.ShapeDtypeStruct
+        moved = (experts, per_holder, width)
+        sums, own_mean, own_square, scales, live = pl.pallas_call(
             functools.partial(kernel, levels, experts, pieces, per_holder),
-            out_shape=[jax.ShapeDtypeStruct(own, f32)] * 3 + [jax.ShapeDtypeStruct((maxb, width), f32)] * 3,
-            in_specs=[hbm] * 8 + [smem] * 4,
-            out_specs=[vmem] * 6,
+            out_shape=[pltpu.VMEM(s, f32) for s in (own, blocks, blocks, (3, 128), (maxb, 128))],
+            in_specs=[hbm] * 7 + [pl.BlockSpec(memory_space=pltpu.SMEM)],
+            out_specs=[vmem] * 5,
             scratch_shapes=[
                 pltpu.VMEM((levels, CORES, pieces, size, cols), ag.dtype),
                 pltpu.VMEM((levels, pieces, size, cols), f32),
                 pltpu.VMEM((levels, pieces, size, cols), f32),
                 pltpu.VMEM((2, levels, pieces, size, cols), f32),
-                pltpu.VMEM(own, f32), pltpu.VMEM(own, f32), pltpu.VMEM(own, f32),
-                pltpu.VMEM((maxb, width), f32), pltpu.VMEM((maxb, width), f32),
+                pltpu.VMEM(blocks, f32),
                 pltpu.VMEM((slots, width), f32), pltpu.VMEM((slots, width), f32),
-                pltpu.VMEM((experts, per_holder, width), f32), pltpu.VMEM((experts, per_holder, width), f32),
-                pltpu.VMEM((experts, per_holder, width), f32), pltpu.VMEM((experts, per_holder, width), f32),
-                pltpu.VMEM((maxb, width), f32), pltpu.VMEM((maxb, width), f32),
+                pltpu.VMEM(moved, f32), pltpu.VMEM(moved, f32),
+                pltpu.VMEM(moved, f32), pltpu.VMEM(moved, f32),
                 pltpu.VMEM((1, 128), f32), pltpu.VMEM((n_dp * experts, 1, 128), f32),
-                dma((levels,)), dma((7,)), dma((k,)), dma((k,)), dma((2, k)), dma((2, k)),
+                pltpu.SMEM(count.shape, jnp.int32), pltpu.SMEM(holder.shape, jnp.int32),
+                pltpu.SMEM(slot.shape, jnp.int32),
+                dma((levels,)), dma((6,)), dma((k,)), dma((k,)), dma((2, k)), dma((2, k)),
                 dma((2, experts)), dma((2, experts)), dma((n_dp * experts,)), dma(()),
             ],
             compiler_params=pltpu.CompilerParams(
-                collective_id=0, has_side_effects=True, vmem_limit_bytes=40 * 1024 * 1024
+                collective_id=0, has_side_effects=True, vmem_limit_bytes=LIMIT
             ),
         )(
-            ag.reshape(levels, CORES, pieces, size, cols),
-            aw.reshape(own), am.reshape(own), av.reshape(own),
-            eg[0, 0], ew[0, 0], hm[0], hs[0], count, holder, slot, step,
+            *(pltpu.with_memory_space_constraint(x, pltpu.HBM) for x in (
+                ag.reshape(levels, CORES, pieces, size, cols), eg[0, 0], hm[0], hs[0],
+                count, holder, slot,
+            )),
+            step,
+        )
+        outs = pl.pallas_call(
+            update,
+            out_shape=[shape(own, f32)] * 3 + [shape(blocks, f32)] * 3,
+            in_specs=[vmem] * 10,
+            out_specs=[hbm] * 6,
+            scratch_shapes=[pltpu.VMEM(own, f32)] * 3 + [pltpu.VMEM(blocks, f32)] * 3 + [dma((3, pieces)), dma((3,))],
+            compiler_params=pltpu.CompilerParams(vmem_limit_bytes=16 * 1024 * 1024),
+        )(
+            aw.reshape(own), am.reshape(own), av.reshape(own), sums,
+            eg[0, 0], ew[0, 0], own_mean, own_square, scales, live,
         )
         return tuple(o.reshape(rows, cols) for o in outs[:3]) + tuple(o[None, None] for o in outs[3:])
 

time: 86.4 us -> 70.1 us (0.81)
  local copies, waits for them, and re-layouts: 15.7 us -> 0.02 us
    unnamed x28 -> x10, local copies, waits for them, and re-layouts: 15.7 us -> 0.02 us
    pallas_call x1, Pallas kernels: 69 us -> 66.1 us  [body(): pl.pallas_call(functools.partial(kernel, levels, experts, pieces, per_hol...]
    pallas_call x0 -> x1, Pallas kernels: none -> 2.22 us  [body(): pl.pallas_call(update, out_shape=[shape(own, f32)] * 3 + [shape(blocks, f...]
where the time goes in v2:
time: 70.1 us; the launch traced here: 69.9 us
  Pallas kernels  68.4 us (98%)
  between operations  1.52 us (2%)
    pallas_call x1, Pallas kernels, body(): pl.pallas_call(functools.partial(kernel, levels, experts, pieces, per_hol...  66.1 us
    pallas_call x1, Pallas kernels, body(): pl.pallas_call(update, out_shape=[shape(own, f32)] * 3 + [shape(blocks, f...  2.22 us

profile of v2, /device:TPU:0, one launch (start us, length us, event | category | flops | bytes accessed | tf_op | source)
XLA Modules:
  0.0 69.9 jit_solution(6530338676164744418)
XLA Ops:
  0.6 0.0 copy-start.4
  0.6 0.0 copy-start
  0.7 0.0 copy-start.3
  0.7 0.0 copy-start.2
  0.7 0.0 copy-start.1
  1.5 66.1 %shard_map.163 = (f32[8,96,256]{2,1,0:T(8,128)S(1)}, f32[8,6144]{1,0:T(8,128)S(1)}, f32[8,6144]{1,0:T(8,128)S(1)}, f32[3,128]{1,0:T(4,128)S(1)}, f32[8,128]{1,0:T(8,128)S(1)}) custom-call(bf16[4,2,8,96,256]{4,3,2,1,0:T(8,128)(2,1)} %bitcast.20, f32[8,6144]{1,0:T(8,128)} %bitcast.14, f32[8,6144]{1,0:T(8,128)} %bitcast.21, f32[8,6144]{1,0:T(8,128)} %bitcast.22, ...), custom_call_target="tpu_custom_call" | custom-call | tf_op jit(solution)/shard_map/pallas_call | solution.py:396
  67.6 0.0 copy-done.4
  67.6 0.0 copy-done
  67.6 0.0 copy-done.3
  67.7 0.0 copy-done.2
  67.7 0.0 copy-done.1
  67.7 2.2 %shard_map.164 = (f32[8,96,256]{2,1,0:T(8,128)}, f32[8,96,256]{2,1,0:T(8,128)}, f32[8,96,256]{2,1,0:T(8,128)}, f32[8,6144]{1,0:T(8,128)}, f32[8,6144]{1,0:T(8,128)}, /*index=5*/f32[8,6144]{1,0:T(8,128)}) custom-call(f32[8,96,256]{2,1,0:T(8,128)S(1)} %bitcast.16, f32[8,96,256]{2,1,0:T(8,128)S(1)} %bitcast.17, f32[8,96,256]{2,1,0:T(8,128)S(1)} %bitcast.18, ...), custom_call_target="tpu_custom_call" | custom-call | tf_op jit(solution)/shard_map/pallas_call | solution.py:426
Async XLA Ops:
  0.6 67.0 %copy-start.4 = (f32[1,1,8,6144]{3,2,1,0:T(8,128)S(1)}, f32[1,1,8,6144]{3,2,1,0:T(8,128)}, u32[]{:S(2)}) copy-start(f32[1,1,8,6144]{3,2,1,0:T(8,128)} %param.17) | copy-start | bytes 589828
  0.6 67.0 %copy-start = (f32[1,1,8,6144]{3,2,1,0:T(8,128)S(1)}, f32[1,1,8,6144]{3,2,1,0:T(8,128)}, u32[]{:S(2)}) copy-start(f32[1,1,8,6144]{3,2,1,0:T(8,128)} %param.16) | copy-start | bytes 589828
  0.7 67.0 %copy-start.3 = (f32[768,256]{1,0:T(8,128)S(1)}, f32[768,256]{1,0:T(8,128)}, u32[]{:S(2)}) copy-start(f32[768,256]{1,0:T(8,128)} %param.15) | copy-start | bytes 2359300
  0.7 67.0 %copy-start.2 = (f32[768,256]{1,0:T(8,128)S(1)}, f32[768,256]{1,0:T(8,128)}, u32[]{:S(2)}) copy-start(f32[768,256]{1,0:T(8,128)} %param.14) | copy-start | bytes 2359300
  0.7 67.0 %copy-start.1 = (f32[768,256]{1,0:T(8,128)S(1)}, f32[768,256]{1,0:T(8,128)}, u32[]{:S(2)}) copy-start(f32[768,256]{1,0:T(8,128)} %param.13) | copy-start | bytes 2359300

commit v3 on v2

--- a/solution.py
+++ b/solution.py
@@ -9,7 +9,7 @@
 
 MESH = pl.DeviceIdType.MESH
 CORES = 2
-LAG = 3
+LAG = 1
 LIMIT = 40 * 1024 * 1024
 
 beta_first = 0.9
@@ -44,9 +44,9 @@
 
 def kernel(
     levels, experts, pieces, per_holder,
-    grad_hbm, eg_hbm, hm_hbm, hs_hbm, count_hbm, holder_hbm, slot_hbm, step_ref,
-    sum_ref, own_mean, own_square, scale_ref, live_ref,
-    grad, pair_out, local, recv, eg, hm, hs,
+    grad_hbm, eg_hbm, ew_hbm, w_hbm, m_hbm, v_hbm, hm_hbm, hs_hbm, count_hbm, holder_hbm, slot_hbm, step_ref,
+    sum_ref, own_mean, own_square, scale_ref, live_ref, eg, ew, w_in, m_in, v_in,
+    grad, pair_out, local, recv, hm, hs,
     out_mean, out_square, in_mean, in_square, part, parts, count_ref, holder_ref, slot_ref,
     grad_sem, load_sem, pair_send, pair_recv, link_send, link_recv,
     mom_send, mom_recv, part_send, part_recv,
@@ -77,12 +77,10 @@
             (
                 (count_hbm, count_ref), (holder_hbm, holder_ref), (slot_hbm, slot_ref),
                 (hm_hbm, hm), (hs_hbm, hs), (eg_hbm, eg),
+                (ew_hbm, ew), (w_hbm, w_in), (m_hbm, m_in), (v_hbm, v_in),
             )
         )
     ]
-    for load in loads:
-        load.start()
-
     barrier = pltpu.get_barrier_semaphore()
     pl.semaphore_signal(barrier, inc=1, device_id=(partner, me), device_id_type=MESH)
     for off in range(1, experts):
@@ -148,6 +146,9 @@
     def _(p):
         pair_copy(first, p).start()
 
+    for load in loads[:5]:
+        load.start()
+
     @pl.loop(0, levels)
     def _(j):
         @pl.when(j + 1 < levels)
@@ -156,6 +157,8 @@
 
         take(j)
 
+    for load in loads[5:]:
+        load.start()
     for load in loads[:5]:
         load.wait()
 
@@ -227,7 +230,8 @@
         rank = jnp.minimum(rank, per_holder - 1)
         own_mean[pl.ds(b, 1), :] = in_mean[holder, pl.ds(rank, 1), :]
         own_square[pl.ds(b, 1), :] = in_square[holder, pl.ds(rank, 1), :]
-    loads[5].wait()
+    for load in loads[5:]:
+        load.wait()
     width = eg.shape[1]
     live = lax.broadcasted_iota(jnp.int32, (maxb, 128), 0) < owned
     acc = jnp.zeros((maxb, 128), jnp.float32)
@@ -365,7 +369,7 @@
 
 
 def piece_rows(rows):
-    for size in range(96, 0, -16):
+    for size in range(192, 0, -16):
         if rows % size == 0:
             return size
     return rows
@@ -393,24 +397,23 @@
         blocks = (maxb, width)
         shape = jax.ShapeDtypeStruct
         moved = (experts, per_holder, width)
-        sums, own_mean, own_square, scales, live = pl.pallas_call(
+        sums, own_mean, own_square, scales, live, eg_in, ew_in, w_in, m_in, v_in = pl.pallas_call(
             functools.partial(kernel, levels, experts, pieces, per_holder),
-            out_shape=[pltpu.VMEM(s, f32) for s in (own, blocks, blocks, (3, 128), (maxb, 128))],
-            in_specs=[hbm] * 7 + [pl.BlockSpec(memory_space=pltpu.SMEM)],
-            out_specs=[vmem] * 5,
+            out_shape=[pltpu.VMEM(s, f32) for s in (own, blocks, blocks, (3, 128), (maxb, 128), blocks, blocks, own, own, own)],
+            in_specs=[hbm] * 11 + [pl.BlockSpec(memory_space=pltpu.SMEM)],
+            out_specs=[vmem] * 10,
             scratch_shapes=[
                 pltpu.VMEM((levels, CORES, pieces, size, cols), ag.dtype),
                 pltpu.VMEM((levels, pieces, size, cols), f32),
                 pltpu.VMEM((levels, pieces, size, cols), f32),
                 pltpu.VMEM((2, levels, pieces, size, cols), f32),
-                pltpu.VMEM(blocks, f32),
                 pltpu.VMEM((slots, width), f32), pltpu.VMEM((slots, width), f32),
                 pltpu.VMEM(moved, f32), pltpu.VMEM(moved, f32),
                 pltpu.VMEM(moved, f32), pltpu.VMEM(moved, f32),
                 pltpu.VMEM((1, 128), f32), pltpu.VMEM((n_dp * experts, 1, 128), f32),
                 pltpu.SMEM(count.shape, jnp.int32), pltpu.SMEM(holder.shape, jnp.int32),
                 pltpu.SMEM(slot.shape, jnp.int32),
-                dma((levels,)), dma((6,)), dma((k,)), dma((k,)), dma((2, k)), dma((2, k)),
+                dma((levels,)), dma((10,)), dma((k,)), dma((k,)), dma((2, k)), dma((2, k)),
                 dma((2, experts)), dma((2, experts)), dma((n_dp * experts,)), dma(()),
             ],
             compiler_params=pltpu.CompilerParams(
@@ -418,7 +421,8 @@
             ),
         )(
             *(pltpu.with_memory_space_constraint(x, pltpu.HBM) for x in (
-                ag.reshape(levels, CORES, pieces, size, cols), eg[0, 0], hm[0], hs[0],
+                ag.reshape(levels, CORES, pieces, size, cols), eg[0, 0], ew[0, 0],
+                aw.reshape(own), am.reshape(own), av.reshape(own), hm[0], hs[0],
                 count, holder, slot,
             )),
             step,
@@ -431,8 +435,7 @@
             scratch_shapes=[pltpu.VMEM(own, f32)] * 3 + [pltpu.VMEM(blocks, f32)] * 3 + [dma((3, pieces)), dma((3,))],
             compiler_params=pltpu.CompilerParams(vmem_limit_bytes=16 * 1024 * 1024),
         )(
-            aw.reshape(own), am.reshape(own), av.reshape(own), sums,
-            eg[0, 0], ew[0, 0], own_mean, own_square, scales, live,
+            w_in, m_in, v_in, sums, eg_in, ew_in, own_mean, own_square, scales, live,
         )
         return tuple(o.reshape(rows, cols) for o in outs[:3]) + tuple(o[None, None] for o in outs[3:])
 

time: 70.1 us -> 68.9 us (0.983)
  Pallas kernels: 68.4 us -> 67.4 us
    pallas_call x1, Pallas kernels: 66.1 us -> 65.2 us  [body(): pl.pallas_call(functools.partial(kernel, levels, experts, pieces, per_hol...]
where the time goes in v3:
time: 68.9 us; the launch traced here: 68.7 us
  Pallas kernels  67.4 us (98%)
  between operations  1.29 us (2%)
    pallas_call x1, Pallas kernels, body(): pl.pallas_call(functools.partial(kernel, levels, experts, pieces, per_hol...  65.2 us
    pallas_call x1, Pallas kernels, body(): pl.pallas_call(update, out_shape=[shape(own, f32)] * 3 + [shape(blocks, f...  2.17 us

profile of v3, /device:TPU:0, one launch (start us, length us, event | category | flops | bytes accessed | tf_op | source)
XLA Modules:
  0.0 68.7 jit_solution(2582337378435924622)
XLA Ops:
  1.3 65.2 %shard_map.163 = (f32[4,192,256]{2,1,0:T(8,128)S(1)}, f32[8,6144]{1,0:T(8,128)S(1)}, f32[8,6144]{1,0:T(8,128)S(1)}, f32[3,128]{1,0:T(4,128)S(1)}, f32[8,128]{1,0...) custom-call(bf16[4,2,4,192,256]{4,3,2,1,0:T(8,128)(2,1)} %bitcast.14, ...), custom_call_target="tpu_custom_call" | custom-call | tf_op jit(solution)/shard_map/pallas_call | solution.py:400
  66.5 2.2 %shard_map.164 = (f32[4,192,256]{2,1,0:T(8,128)}, f32[4,192,256]{2,1,0:T(8,128)}, f32[4,192,256]{2,1,0:T(8,128)}, f32[8,6144]{1,0:T(8,128)}, f32[8,6144]{1,0:T(8,128)}, /*index=5*/f32[8,6144]{1,0:T(8,128)}) custom-call(f32[4,192,256]{2,1,0:T(8,128)S(1)} %get-tuple-element.22.w_in, f32[4,192,256]{2,1,0:T(8,128)S(1)} %get-tuple-element.23.m_in, ...), custom_call_target="tpu_custom_call" | custom-call | tf_op jit(solution)/shard_map/pallas_call | solution.py:430
